TPU v7x, 32 devices: a whole 2x2x4 slice. The times are simulated.
32 devices in a mesh: bank: 4 (over x, core), zero: 8 (over z, y).
Axes of the slice: x: 2, y: 2, z: 4, core: 2. Of those that a mesh axis runs over, the one named last changes fastest.
Arguments:
- w_gate: float32 [64, 2048, 1024], P('bank', 'zero'), may hold values from -0.1875 to 0.1875
- avg_gate: float32 [64, 2048, 1024], P('bank', 'zero'), may hold values from -0.125 to 0.125
- w_up: float32 [64, 2048, 1024], P('bank', 'zero'), may hold values from -0.1875 to 0.1875
- avg_up: float32 [64, 2048, 1024], P('bank', 'zero'), may hold values from -0.125 to 0.125
- mix_share: float32 [64], P('bank'), may hold values from 0.2 to 0.8
- router_weight: float32 [2048, 64], P('zero', 'bank'), may hold values from -0.125 to 0.125
- router_gain: float32 [2048], P('zero'), may hold values from 0.25 to 1.75
Outputs:
- serve_gate: bfloat16 [64, 2048, 1024], P('bank', None, 'zero')
- serve_up: bfloat16 [64, 2048, 1024], P('bank', None, 'zero')
- scale_gate: float32 [64, 1024], P('bank', 'zero')
- scale_up: float32 [64, 1024], P('bank', 'zero')
- serve_router: bfloat16 [2048, 64], replicated
All inputs are finite; a program needn't handle non-finite values. Where the computation divides by a largest or mean magnitude, that divisor is 1e-20 or more.
Results may differ from a plain program's by a relative error of at most 0.001.
Values may be sent and summed in bfloat16 or wider, within the bound.
A program may use at most 256 MiB of HBM per device.

v0:
```python
import jax
import jax.numpy as jnp
from jax import lax
from jax.sharding import PartitionSpec as P

D_MODEL = 2048


def on_device(w_gate, avg_gate, w_up, avg_up, mix_share, router_weight, router_gain):
    fresh_gate = mix_share[:, None, None] * w_gate + (1.0 - mix_share[:, None, None]) * avg_gate
    fresh_up = mix_share[:, None, None] * w_up + (1.0 - mix_share[:, None, None]) * avg_up
    total_gate, total_up = lax.psum(
        (jnp.sum(jnp.abs(fresh_gate), axis=1), jnp.sum(jnp.abs(fresh_up), axis=1)), "zero"
    )
    scale_gate = total_gate / D_MODEL
    scale_up = total_up / D_MODEL
    narrow_gate, narrow_up = (
        (fresh_gate / jnp.expand_dims(scale_gate, 1)).astype(jnp.bfloat16),
        (fresh_up / jnp.expand_dims(scale_up, 1)).astype(jnp.bfloat16),
    )
    serve_gate, serve_up = (
        lax.all_to_all(narrow_gate, "zero", split_axis=2, concat_axis=1, tiled=True),
        lax.all_to_all(narrow_up, "zero", split_axis=2, concat_axis=1, tiled=True),
    )
    scale_gate = lax.dynamic_slice_in_dim(
        scale_gate, lax.axis_index("zero") * serve_gate.shape[2], serve_gate.shape[2], axis=1
    )
    scale_up = lax.dynamic_slice_in_dim(
        scale_up, lax.axis_index("zero") * serve_up.shape[2], serve_up.shape[2], axis=1
    )
    part_router = (router_weight * router_gain[:, None]).astype(jnp.bfloat16)
    row_router = lax.all_gather(part_router, "zero", axis=0, tiled=True)
    serve_router = lax.all_gather(row_router, "bank", axis=1, tiled=True)
    return (serve_gate, serve_up, scale_gate, scale_up, serve_router)


def solution(mesh):
    in_specs = (
        P("bank", "zero", None),
        P("bank", "zero", None),
        P("bank", "zero", None),
        P("bank", "zero", None),
        P("bank"),
        P("zero", "bank"),
        P("zero"),
    )
    out_specs = (
        P("bank", None, "zero"),
        P("bank", None, "zero"),
        P("bank", "zero"),
        P("bank", "zero"),
        P(),
    )
    return jax.shard_map(
        on_device, mesh=mesh, in_specs=in_specs, out_specs=out_specs, check_vma=False
    )
```

profile of v0, /device:TPU:0, one launch (start us, length us, event | category | flops | bytes accessed | tf_op | source)
XLA Modules:
  0.0 642.4 jit_solution(310486662684483789)
XLA Ops:
  7.2 0.0 all-reduce.3.cloned.1.call-start
  7.2 17.6 %copy.22 = f32[16,256,1024]{1,0,2:T(8,128)} copy(f32[16,256,1024]{2,1,0:T(8,128)} %param.7) | data formatting | bytes 33554432 | tf_op args[0]
  24.8 17.6 %copy.23 = f32[16,256,1024]{1,0,2:T(8,128)} copy(f32[16,256,1024]{2,1,0:T(8,128)} %param.8) | data formatting | bytes 33554432 | tf_op args[1]
  42.4 17.6 %copy.25 = f32[16,256,1024]{1,0,2:T(8,128)} copy(f32[16,256,1024]{2,1,0:T(8,128)} %param.9) | data formatting | bytes 33554432 | tf_op args[2]
  60.0 0.0 copy-start.1
  60.0 17.6 %copy.26 = f32[16,256,1024]{1,0,2:T(8,128)} copy(f32[16,256,1024]{2,1,0:T(8,128)} %param.10) | data formatting | bytes 33554432 | tf_op args[3]
  77.6 0.0 copy-done.1
  77.6 23.7 %abs_reduce_fusion = (f32[16,1024]{0,1:T(8,128)}, f32[16,1024]{0,1:T(8,128)}) fusion(f32[16,256,1024]{1,0,2:T(8,128)} %copy.26, f32[16]{0:T(128)S(1)} %broadcast_subtract_fusion, f32[16,256,1024]{1,0,2:T(8,128)} %copy.25, f32[16]{0:T(128)S(1)} %copy-done.1, f32[16,256,1024]{1,0,2:T(8,128)} %copy.23, f32[16,256,1024]{1,0,2:T(8,128)} %copy.22), kind=kLoop, calls=%fused_computation.1 | loop fusion | flops 41910272 | bytes 67240064 | tf_op jit(solution)/shard_map/reduce_sum | solution.py:13
  101.3 0.0 all-reduce.3.cloned.1.call-update
  101.4 81.1 %all-reduce.3.cloned.1.call-done = (f32[16,1024]{0,1:T(8,128)}, f32[16,1024]{0,1:T(8,128)}) async-done(((f32[16,1024]{0,1:T(8,128)}, f32[16,1024]{0,1:T(8,128)}), (f32[16,1024]{0,1:T(8,128)}, f32[16,1024]{0,1:T(8,128)})) %all-reduce.3.cloned.1.call-update) | async-done | bytes 131088 | tf_op jit(solution)/shard_map/psum | solution.py:12
  182.5 1.3 broadcast_multiply_fusion
  183.8 25.3 %divide_convert_fusion = (bf16[16,256,1024]{1,0,2:T(8,128)(2,1)}, bf16[16,256,1024]{1,0,2:T(8,128)(2,1)S(1)}) fusion(f32[16,1024]{0,1:T(8,128)S(1)} %get-tuple-element.16, f32[16,256,1024]{1,0,2:T(8,128)} %copy.26, f32[16]{0:T(128)S(1)} %broadcast_subtract_fusion, f32[16,256,1024]{1,0,2:T(8,128)} %copy.25, f32[16]{0:T(128)S(1)} %copy-done.1, ...), kind=kLoop, calls=%fused_computation | loop fusion | flops 41943040 | bytes 84017280 | tf_op jit(solution)/shard_map/convert_element_type | solution.py:19
  209.1 0.0 copy-start
  209.1 0.0 copy-start.2
  209.1 187.1 %all_to_all.36 = bf16[16,256,1024]{1,0,2:T(8,128)(2,1)} all-to-all(bf16[16,256,1024]{1,0,2:T(8,128)(2,1)S(1)} %get-tuple-element.15), channel_id=1, replica_groups=mesh['bank'=4,'zero'=8] {'zero'}, dimensions={2} | all-to-all | bytes 16777216 | tf_op jit(solution)/shard_map/all_to_all | solution.py:22
  396.2 4.9 all-to-all-start.1
  401.1 0.0 copy-done
  401.1 0.0 copy-done.2
  401.1 202.0 %all_gather.6 = bf16[2048,16]{0,1:T(8,128)(2,1)S(1)} all-gather(bf16[256,16]{0,1:T(8,128)(2,1)S(1)} %multiply_convert_fusion), channel_id=1, replica_groups=mesh['bank'=4,'zero'=8] {'zero'}, dimensions={0}, use_global_device_ids=true | all-gather | bytes 73728 | tf_op jit(solution)/shard_map/all_gather | solution.py:32
  603.2 5.8 all_gather.7
  608.9 0.7 copy.28
  609.6 0.7 copy.29
  610.3 12.3 %copy.24 = bf16[16,8,256,128]{3,2,1,0:T(8,128)(2,1)} copy(bf16[16,8,256,128]{2,0,3,1:T(8,128)(2,1)} %bitcast.8) | data formatting | bytes 16777216 | tf_op jit(solution)/shard_map/all_to_all | solution.py:22
  622.6 0.0 all-to-all-done.1
  622.6 12.3 %copy.27 = bf16[16,8,256,128]{3,2,1,0:T(8,128)(2,1)} copy(bf16[16,8,256,128]{2,0,3,1:T(8,128)(2,1)} %bitcast.4) | data formatting | bytes 16777216 | tf_op jit(solution)/shard_map/all_to_all | solution.py:23
  634.8 0.7 copy.33
  (4 shorter events, 0.0 us)
Async XLA Ops:
  7.2 175.3 %all-reduce.3.cloned.1.call-start = ((), (), s32[]{:S(2)}) async-start(), calls=%async_computation.2 | async-start | bytes 2097152 | tf_op jit(solution)/shard_map/psum | solution.py:12
  60.0 17.6 %copy-start.1 = (f32[16]{0:T(128)S(1)}, f32[16]{0:T(128)}, u32[]{:S(2)}) copy-start(f32[16]{0:T(128)} %param.11) | copy-start | bytes 196
  209.1 192.0 %copy-start = (f32[256,16]{0,1:T(8,128)S(1)}, f32[256,16]{0,1:T(8,128)}, u32[]{:S(2)}) copy-start(f32[256,16]{0,1:T(8,128)} %param.12) | copy-start | bytes 49156
  209.1 192.0 %copy-start.2 = (f32[256]{0:T(256)S(1)}, f32[256]{0:T(256)}, u32[]{:S(2)}) copy-start(f32[256]{0:T(256)} %param.13) | copy-start | bytes 3076
  396.2 226.4 %all-to-all-start.1 = ((bf16[16,256,1024]{1,0,2:T(8,128)(2,1)}), bf16[16,256,1024]{1,0,2:T(8,128)(2,1)}, u32[]{:S(2)}, u32[]{:S(2)}) async-start(bf16[16,256,1024]{1,0,2:T(8,128)(2,1)} %get-tuple-element.14), calls=%async_computation.1 | async-start | bytes 16777216 | tf_op jit(solution)/shard_map/all_to_all | solution.py:23
Sparse Core Ops, SparseCore 0:
  101.5 80.9 all-reduce.2
where the time goes:
time: 644 us; the launch traced here: 642 us
  blocking collectives  395 us (61%)
  local copies, waits for them, and re-layouts  97 us (15%)
  waiting for transfers between devices  81.2 us (13%)
  other arithmetic  50.3 us (8%)
  between operations  14.1 us (2%)
    all_gather x1, blocking collectives, on_device(): row_router = lax.all_gather(part_router, 'zero', axis=0, tiled=True)  202 us
    all_to_all x1, blocking collectives, on_device(): lax.all_to_all(narrow_gate, 'zero', split_axis=2, concat_axis=1, tiled=True)  187 us
    psum x1, waiting for transfers between devices, on_device(): lax.psum((jnp.sum(jnp.abs(fresh_gate), axis=1), jnp.sum(jnp.abs(fresh_up)...  81.1 us
    unnamed x13, local copies, waits for them, and re-layouts  72.5 us
    convert_element_type x1, other arithmetic, on_device(): (fresh_up / jnp.expand_dims(scale_up, 1)).astype(jnp.bfloat16)  25.3 us
    reduce_sum x1, other arithmetic, on_device(): jnp.sum(jnp.abs(fresh_up), axis=1)  23.7 us
  transfers between devices with their start and end apart: 2, of which 1 were waited for; matrix products, arithmetic and copies ran while one was open for 2% of the time, Pallas kernels for 0%

commit v1 on v0

--- a/solution.py
+++ b/solution.py
@@ -18,8 +18,21 @@
         (fresh_gate / jnp.expand_dims(scale_gate, 1)).astype(jnp.bfloat16),
         (fresh_up / jnp.expand_dims(scale_up, 1)).astype(jnp.bfloat16),
     )
+
+    def view_the_leaf(x_local, net_axis):
+        z = jnp.concatenate(
+            jax.lax.all_to_all(
+                jnp.stack(jnp.split(x_local, jax.lax.axis_size(net_axis), 2), axis=0),
+                axis_name=net_axis,
+                split_axis=0,
+                concat_axis=0,
+            ),
+            axis=1,
+        )
+        return z
+
     serve_gate, serve_up = (
-        lax.all_to_all(narrow_gate, "zero", split_axis=2, concat_axis=1, tiled=True),
+        view_the_leaf(narrow_gate, "zero"),
         lax.all_to_all(narrow_up, "zero", split_axis=2, concat_axis=1, tiled=True),
     )
     scale_gate = lax.dynamic_slice_in_dim(

time: 644 us -> 577 us (0.90)
  blocking collectives: 395 us -> 208 us
  waiting for transfers between devices: 81.2 us -> 240 us
  local copies, waits for them, and re-layouts: 97 us -> 49.8 us
    all_to_all x1 -> x0, blocking collectives: 187 us -> none  [on_device(): lax.all_to_all(narrow_gate, 'zero', split_axis=2, concat_axis=1, tiled=True)]
    all_to_all x1, waiting for transfers between devices: 0.01 us -> 166 us  [on_device(): lax.all_to_all(narrow_up, 'zero', split_axis=2, concat_axis=1, tiled=True)]
    unnamed x13 -> x16, local copies, waits for them, and re-layouts: 72.5 us -> 14.6 us
    convert_element_type x0 -> x1, local copies, waits for them, and re-layouts: none -> 12.6 us  [on_device(): (fresh_up / jnp.expand_dims(scale_up, 1)).astype(jnp.bfloat16)]
    psum x1, waiting for transfers between devices: 81.1 us -> 73.6 us  [on_device(): lax.psum((jnp.sum(jnp.abs(fresh_gate), axis=1), jnp.sum(jnp.abs(fresh_up)...]
  transfers between devices with their start and end apart: 2 -> 3, of which waited for: 1 -> 2; matrix products, arithmetic and copies ran while one was open for 2% -> 5% of each run, Pallas kernels for 0% -> 0%
where the time goes in v1:
time: 577 us; the launch traced here: 576 us
  waiting for transfers between devices  240 us (42%)
  blocking collectives  208 us (36%)
  other arithmetic  54.3 us (9%)
  local copies, waits for them, and re-layouts  49.8 us (9%)
  between operations  14.1 us (2%)
  starting transfers between devices  9.99 us (2%)
    all_gather x1, blocking collectives, on_device(): row_router = lax.all_gather(part_router, 'zero', axis=0, tiled=True)  202 us
    all_to_all x1, waiting for transfers between devices, on_device(): lax.all_to_all(narrow_up, 'zero', split_axis=2, concat_axis=1, tiled=True)  166 us
    psum x1, waiting for transfers between devices, on_device(): lax.psum((jnp.sum(jnp.abs(fresh_gate), axis=1), jnp.sum(jnp.abs(fresh_up)...  73.6 us
    convert_element_type x1, other arithmetic, on_device(): (fresh_up / jnp.expand_dims(scale_up, 1)).astype(jnp.bfloat16)  29.4 us
    reduce_sum x1, other arithmetic, on_device(): jnp.sum(jnp.abs(fresh_up), axis=1)  23.3 us
    unnamed x16, local copies, waits for them, and re-layouts  14.6 us
    convert_element_type x1, local copies, waits for them, and re-layouts, on_device(): (fresh_up / jnp.expand_dims(scale_up, 1)).astype(jnp.bfloat16)  12.6 us
    all_to_all x1, local copies, waits for them, and re-layouts, on_device(): lax.all_to_all(narrow_up, 'zero', split_axis=2, concat_axis=1, tiled=True)  12.3 us
  transfers between devices with their start and end apart: 3, of which 2 were waited for; matrix products, arithmetic and copies ran while one was open for 5% of the time, Pallas kernels for 0%

profile of v1, /device:TPU:0, one launch (start us, length us, event | category | flops | bytes accessed | tf_op | source)
XLA Modules:
  0.0 575.6 jit_solution(11192683282633137872)
XLA Ops:
  7.2 0.0 all-reduce.3.cloned.1.call-start
  7.2 0.7 broadcast_subtract_fusion
  7.9 23.3 %abs_reduce_fusion = (f32[16,1024]{1,0:T(8,128)}, f32[16,1024]{1,0:T(8,128)}) fusion(f32[16,256,1024]{2,1,0:T(8,128)} %param.10, f32[16]{0:T(128)S(1)} %broadcast_subtract_fusion, f32[16,256,1024]{2,1,0:T(8,128)} %param.9, f32[16]{0:T(128)} %param.11, f32[16,256,1024]{2,1,0:T(8,128)} %param.8, f32[16,256,1024]{2,1,0:T(8,128)} %param.7), kind=kLoop, calls=%fused_computation.1 | loop fusion | flops 41910272 | bytes 67240064 | tf_op jit(solution)/shard_map/reduce_sum | solution.py:13
  31.2 0.0 all-reduce.3.cloned.1.call-update
  31.2 73.6 %all-reduce.3.cloned.1.call-done = (f32[16,1024]{1,0:T(8,128)}, f32[16,1024]{1,0:T(8,128)}) async-done(((f32[16,1024]{1,0:T(8,128)}, f32[16,1024]{1,0:T(8,128)}), (f32[16,1024]{1,0:T(8,128)}, f32[16,1024]{1,0:T(8,128)})) %all-reduce.3.cloned.1.call-update) | async-done | bytes 131088 | tf_op jit(solution)/shard_map/psum | solution.py:12
  104.8 0.9 broadcast_multiply_fusion
  105.7 0.0 copy-done.2
  105.7 29.4 %divide_convert_fusion = (bf16[16,256,1024]{2,1,0:T(8,128)(2,1)}, bf16[16,256,1024]{2,1,0:T(8,128)(2,1)}) fusion(f32[16,1024]{1,0:T(8,128)S(1)} %get-tuple-element.11, f32[16,256,1024]{2,1,0:T(8,128)} %param.10, f32[16]{0:T(128)S(1)} %broadcast_subtract_fusion, f32[16,256,1024]{2,1,0:T(8,128)} %param.9, f32[16]{0:T(128)S(1)} %copy-done.2, ...), kind=kLoop, calls=%fused_computation | loop fusion | flops 41943040 | bytes 84017280 | tf_op jit(solution)/shard_map/convert_element_type | solution.py:19
  135.1 12.6 %copy.31 = bf16[16,256,1024]{1,0,2:T(8,128)(2,1)} copy(bf16[16,256,1024]{2,1,0:T(8,128)(2,1)} %get-tuple-element.9) | data formatting | bytes 16777216 | tf_op jit(solution)/shard_map/convert_element_type | solution.py:19
  147.7 4.9 all-to-all-start.1
  152.6 0.0 copy-start
  152.6 2.4 fusion.7
  155.1 3.0 fusion.6
  158.1 2.3 fusion.5
  160.4 2.3 fusion.4
  162.7 0.0 copy-done
  162.7 1.2 fusion.3
  163.9 1.3 fusion.2
  165.2 1.3 fusion.1
  166.5 1.3 fusion
  167.8 166.2 %all-to-all-done.1 = bf16[16,256,1024]{1,0,2:T(8,128)(2,1)} async-done(((bf16[16,256,1024]{1,0,2:T(8,128)(2,1)}), bf16[16,256,1024]{1,0,2:T(8,128)(2,1)}, u32[]{:S(2)}, u32[]{:S(2)}) %all-to-all-start.1) | async-done | bytes 8388640 | tf_op jit(solution)/shard_map/all_to_all | solution.py:36
  334.0 5.0 all-to-all-start
  339.0 0.0 copy-done.1
  339.0 0.0 copy-done.3
  339.0 201.9 %all_gather.6 = bf16[2048,16]{0,1:T(8,128)(2,1)S(1)} all-gather(bf16[256,16]{0,1:T(8,128)(2,1)S(1)} %multiply_convert_fusion), channel_id=1, replica_groups=mesh['bank'=4,'zero'=8] {'zero'}, dimensions={0}, use_global_device_ids=true | all-gather | bytes 73728 | tf_op jit(solution)/shard_map/all_gather | solution.py:45
  540.9 5.8 %all_gather.7 = bf16[2048,64]{0,1:T(8,128)(2,1)S(1)} all-gather(bf16[2048,16]{0,1:T(8,128)(2,1)S(1)} %all_gather.6), channel_id=1, replica_groups=mesh['bank'=4,'zero'=8] {'bank'}, dimensions={1}, use_global_device_ids=true | all-gather | bytes 327680 | tf_op jit(solution)/shard_map/all_gather | solution.py:46
  546.7 0.6 constant_dynamic-slice_fusion
  547.3 0.6 constant_dynamic-slice_fusion.1
  547.9 12.3 %copy.32 = bf16[16,8,256,128]{3,2,1,0:T(8,128)(2,1)} copy(bf16[16,8,256,128]{2,0,3,1:T(8,128)(2,1)} %bitcast.11) | data formatting | bytes 16777216 | tf_op jit(solution)/shard_map/all_to_all | solution.py:36
  560.2 0.0 all-to-all-done
  560.2 7.9 %copy.30 = bf16[8,16,256,128]{3,2,0,1:T(8,128)(2,1)} copy(bf16[8,16,256,128]{3,2,1,0:T(8,128)(2,1)} %all-to-all-done) | data formatting | bytes 16777216 | tf_op jit(solution)/shard_map/all_to_all | solution.py:24
  568.1 0.7 copy.43
  (4 shorter events, 0.0 us)
Async XLA Ops:
  7.2 97.6 %all-reduce.3.cloned.1.call-start = ((), (), s32[]{:S(2)}) async-start(), calls=%async_computation.2 | async-start | bytes 262144 | tf_op jit(solution)/shard_map/psum | solution.py:12
  7.9 97.8 %copy-start.2 = (f32[16]{0:T(128)S(1)}, f32[16]{0:T(128)}, u32[]{:S(2)}) copy-start(f32[16]{0:T(128)} %param.11) | copy-start | bytes 196
  147.7 186.3 %all-to-all-start.1 = ((bf16[16,256,1024]{1,0,2:T(8,128)(2,1)}), bf16[16,256,1024]{1,0,2:T(8,128)(2,1)}, u32[]{:S(2)}, u32[]{:S(2)}) async-start(bf16[16,256,1024]{1,0,2:T(8,128)(2,1)} %copy.31), calls=%async_computation.1 | async-start | bytes 16777216 | tf_op jit(solution)/shard_map/all_to_all | solution.py:36
  152.6 10.1 %copy-start = (bf16[16,256,1024]{2,1,0:T(8,128)(2,1)S(1)}, bf16[16,256,1024]{2,1,0:T(8,128)(2,1)}, u32[]{:S(2)}) copy-start(bf16[16,256,1024]{2,1,0:T(8,128)(2,1)} %get-tuple-element.10) | copy-start | bytes 25165828
  167.8 171.2 %copy-start.1 = (f32[256,16]{0,1:T(8,128)S(1)}, f32[256,16]{0,1:T(8,128)}, u32[]{:S(2)}) copy-start(f32[256,16]{0,1:T(8,128)} %param.12) | copy-start | bytes 49156
  167.8 171.2 %copy-start.3 = (f32[256]{0:T(256)S(1)}, f32[256]{0:T(256)}, u32[]{:S(2)}) copy-start(f32[256]{0:T(256)} %param.13) | copy-start | bytes 3076
  334.0 226.2 %all-to-all-start = ((bf16[8,16,256,128]{3,2,1,0:T(8,128)(2,1)}), bf16[8,16,256,128]{3,2,1,0:T(8,128)(2,1)}, u32[]{:S(2)}, u32[]{:S(2)}) async-start(bf16[8,16,256,128]{3,2,1,0:T(8,128)(2,1)} %fusion), calls=%async_computation | async-start | bytes 16777216 | tf_op jit(solution)/shard_map/all_to_all | solution.py:24
Sparse Core Ops, SparseCore 0:
  31.3 73.4 all-reduce.2
